TPU v7x, 32 devices: a whole 2x2x4 slice. The times are simulated.
32 devices in a mesh: curve: 16 (over z, y, core), tm: 2 (over x).
Axes of the slice: x: 2, y: 2, z: 4, core: 2. Of those that a mesh axis runs over, the one named last changes fastest.
Arguments:
- samples: float32 [4096, 65536], P('curve', 'tm'), may hold values from -30 to 30
- smoothing: float32 [4096], P('curve'), may hold values from 0.5 to 20
- test_matrix: float32 [4096, 64], P('tm'), may hold values from -0.75 to 0.75
- sketch_prev: float32 [4096, 64], P('tm', 'curve'), may hold values from -1.2 to 1.2
Outputs:
- coefficients: float32 [4096, 4096], P('curve', 'tm')
- scores: float32 [4096, 64], P('curve')
- sketch: float32 [4096, 64], P('tm', 'curve')
All inputs are finite; a program needn't handle non-finite values.
Results may differ from a plain program's by a relative error of at most 0.0002.
Values sent between devices are 32-bit elements; how exact they have to be, the bound alone decides.
No kernel may reach another device: no remote copies, remote signals or barrier semaphores. Data moves between devices by JAX's collectives and lax.ppermute only.
A program may use at most 192 MiB of HBM per device.

v0:
```python
import jax
import jax.numpy as jnp
from jax import lax
from jax.sharding import PartitionSpec as P

SPB = 16
ITERS = 4
damping = 0.45


def passed_along(block, axis, distance):
    devices = range(lax.axis_size(axis))
    route = [(i - distance, i) for i in devices if i - distance in devices]
    return lax.ppermute(block, axis, route)


def padded_2(block, sides, width):
    for axis, dim in sides:
        count = lax.axis_size(axis)
        forward = [(i, i + 1) for i in range(count - 1)]
        backward = [(target, source) for source, target in forward]
        low = lax.ppermute(
            lax.slice_in_dim(block, block.shape[dim] - width, None, axis=dim), axis, forward
        )
        high = lax.ppermute(lax.slice_in_dim(block, 0, width, axis=dim), axis, backward)
        block = jnp.concatenate([low, block, high], axis=dim)
    return block


def weight_table():
    frac = (jnp.arange(SPB, dtype=jnp.float32) + 0.5) / SPB
    pieces = [
        frac**3 / 6.0,
        (-3.0 * frac**3 + 3.0 * frac**2 + 3.0 * frac + 1.0) / 6.0,
        (3.0 * frac**3 - 6.0 * frac**2 + 4.0) / 6.0,
        (1.0 - frac) ** 3 / 6.0,
    ]
    return jnp.stack(pieces) / SPB


def relax_sweep(widened, target, smooth_col, index_wide, total_basis):
    second = widened[:, 2:] - 2.0 * widened[:, 1:-1] + widened[:, :-2]
    in_range = (index_wide[:-2] >= 0) & (index_wide[:-2] <= total_basis - 3)
    second = jnp.where(in_range[None, :], second, 0.0)
    bending = second[:, 2:] - 2.0 * second[:, 1:-1] + second[:, :-2]
    interior = widened[:, 2:-2]
    column_index = index_wide[2:-2]
    penalty_diag = (
        (column_index <= total_basis - 3).astype(jnp.float32)
        + 4.0 * ((column_index >= 1) & (column_index <= total_basis - 2)).astype(jnp.float32)
        + (column_index >= 2).astype(jnp.float32)
    )
    return interior + damping * (target - interior - smooth_col * bending) / (
        1.0 + smooth_col * penalty_diag
    )


def body(samples, smoothing, test_matrix, sketch_prev):
    row_count = samples.shape[0]
    basis_width = samples.shape[1] // SPB
    blocks = samples.reshape(row_count, basis_width, SPB)
    segment_sums = jnp.einsum(
        "cgq,mq->mcg", blocks, weight_table(), precision=lax.Precision.HIGHEST
    )
    padded = jnp.pad(segment_sums, ((0, 0), (0, 0), (3, 3)))
    extended = (
        padded[0, :, 0 : basis_width + 3]
        + padded[1, :, 1 : basis_width + 4]
        + padded[2, :, 2 : basis_width + 5]
        + padded[3, :, 3 : basis_width + 6]
    )
    spilled = extended[:, basis_width:]
    arrived = passed_along(spilled, "tm", 1)
    proj = jnp.concatenate([extended[:, :3] + arrived, extended[:, 3:basis_width]], axis=1)
    total_basis = basis_width * lax.axis_size("tm")
    first_column = lax.axis_index("tm") * basis_width
    smooth_col = smoothing[:, None]
    margin = 2 * ITERS
    proj_wide = padded_2(proj, (("tm", 1),), margin)
    coefficients = proj_wide
    for sweep_number in range(ITERS):
        margin_now = margin - 2 * sweep_number
        index_wide = (
            first_column - margin_now + jnp.arange(basis_width + 2 * margin_now, dtype=jnp.int32)
        )
        offset = 2 * sweep_number + 2
        target = proj_wide[:, offset : offset + basis_width + 2 * margin_now - 4]
        coefficients = relax_sweep(coefficients, target, smooth_col, index_wide, total_basis)
    curve_total = row_count * lax.axis_size("curve")
    totals = lax.psum(jnp.sum(coefficients, axis=0), "curve")
    column_mean = totals / curve_total
    centered = coefficients - column_mean[None, :]
    partial_value = jnp.dot(
        centered, test_matrix, precision=lax.Precision.HIGHEST, preferred_element_type=jnp.float32
    )
    scores = lax.psum(partial_value, "tm")
    sketch_part = (
        jnp.einsum("ck,cr->kr", centered, scores, precision=lax.Precision.HIGHEST) / curve_total
    )
    owned_part = lax.psum_scatter(sketch_part, "curve", scatter_dimension=1, tiled=True)
    return (coefficients, scores, sketch_prev + owned_part)


def solution(mesh):
    placed = (P("curve", "tm"), P("curve"), P("tm", None), P("tm", "curve"))
    return jax.shard_map(
        body,
        mesh=mesh,
        in_specs=placed,
        out_specs=(P("curve", "tm"), P("curve", None), P("tm", "curve")),
        check_vma=False,
    )
```

profile of v0, /device:TPU:0, one launch (start us, length us, event | category | flops | bytes accessed | tf_op | source)
XLA Modules:
  0.0 307.5 jit_solution(17813712295289506983)
XLA Ops:
  7.2 0.0 copy-start
  7.2 0.0 all-reduce.5.cloned.1.call-start
  7.3 33.5 %copy.12 = f32[256,32768]{0,1:T(8,128)} copy(f32[256,32768]{1,0:T(8,128)} %param.4) | data formatting | bytes 67108864 | tf_op args[0]
  40.7 35.7 %copy.13 = f32[256,2048,16]{1,2,0:T(8,128)} copy(f32[256,2048,16]{0,2,1:T(8,128)} %bitcast.9) | data formatting | bytes 67108864 | tf_op jit(solution)/shard_map/reshape | solution.py:61
  76.4 21.7 %fusion.43 = f32[4,256,2048]{2,0,1:T(4,128)S(1)} fusion(f32[256,2048,16]{1,2,0:T(8,128)} %copy.13, f32[1,16]{1,0:T(1,128)S(1)} %get-tuple-element.11, f32[1,16]{1,0:T(1,128)S(1)} %get-tuple-element.12, f32[1,16]{1,0:T(1,128)S(1)} %get-tuple-element.13, f32[1,16]{1,0:T(1,128)S(1)} %get-tuple-element.14), kind=kOutput, calls=%fused_computation.85 | convolution fusion | flops 402653440 | bytes 41943296 | tf_op jit(solution)/shard_map/cgq,mq->mcg/dot_general | solution.py:62
  98.1 16.1 %fusion.2 = f32[1,256,2051]{2,0,1:T(1,128)S(1)} fusion(f32[4,256,2048]{2,0,1:T(4,128)S(1)} %fusion.43), kind=kLoop, calls=%fused_computation.9 | loop fusion | flops 1575168 | bytes 10488832 | tf_op jit(solution)/shard_map/add | solution.py:67
  114.3 4.1 %copy.14 = f32[1,256,2051]{1,2,0:T(8,128)} copy(f32[1,256,2051]{2,0,1:T(1,128)S(1)} %fusion.2) | data formatting | bytes 4200448 | tf_op jit(solution)/shard_map/add | solution.py:67
  118.4 0.7 slice.196
  119.1 4.9 %collective-permute-start.1 = (f32[256,3]{0,1:T(4,128)S(1)}, f32[256,3]{0,1:T(4,128)S(1)}, u32[]{:S(2)}, u32[]{:S(2)}) collective-permute-start(f32[256,3]{0,1:T(4,128)S(1)} %slice.196), channel_id=1, source_target_pairs={{0,1},{2,3},{4,5},{6,7},{8,9},{10,11},{12,13},{14,15},{16,17},{18,... | collective-permute-start | bytes 9224 | tf_op jit(solution)/shard_map/ppermute | solution.py:14
  124.0 0.7 slice.194
  124.7 1.3 collective-permute-start
  126.0 0.1 convert_add_fusion.2
  126.1 0.1 convert_add_fusion.1
  126.2 0.1 convert_add_fusion
  126.3 0.1 convert_add_fusion.3
  126.3 1.7 slice.197
  128.1 0.0 copy-start.1
  128.1 0.0 collective-permute-done.1
  128.1 0.7 slice_add_fusion.8
  128.9 1.5 collective-permute-start.2
  130.3 0.0 collective-permute-done
  130.4 0.0 copy-done.1
  130.4 4.0 %collective-permute-done.2 = f32[256,8]{0,1:T(8,128)S(1)} collective-permute-done((f32[256,8]{0,1:T(8,128)S(1)}, f32[256,8]{0,1:T(8,128)S(1)}, u32[]{:S(2)}, u32[]{:S(2)}) %collective-permute-start.2) | collective-permute-done | bytes 8224 | tf_op jit(solution)/shard_map/ppermute | solution.py:25
  134.4 5.3 %concatenate.8 = f32[256,2064]{0,1:T(8,128)S(1)} concatenate(f32[256,8]{0,1:T(8,128)S(1)} %collective-permute-done, f32[256,3]{0,1:T(4,128)S(1)} %slice_add_fusion.8, f32[256,2045]{0,1:T(8,128)} %copy-done.1, f32[256,8]{0,1:T(8,128)S(1)} %collective-permute-done.2), dimensions={1} | concatenate | bytes 4227072 | tf_op jit(solution)/shard_map/concatenate | solution.py:26
  139.7 0.0 copy-start.5
  139.7 1.2 fusion.11
  140.9 1.7 fusion.9
  142.6 1.2 fusion.3
  143.8 1.8 fusion.27
  145.6 1.2 fusion.21
  146.8 1.8 fusion.19
  148.6 0.0 copy-start.2
  148.6 1.2 fusion.13
  149.8 0.4 copy-done.2
  150.2 1.8 fusion.56
  152.1 32.6 %psum.14 = f32[2048]{0:T(1024)S(1)} all-reduce(f32[2048]{0:T(1024)S(1)} %get-tuple-element.9), channel_id=1, replica_groups=mesh['curve'=16,'tm'=2] {'curve'}, use_global_device_ids=true, to_apply=%region_1.2 | all-reduce | flops 2048 | bytes 16384 | tf_op jit(solution)/shard_map/psum | solution.py:90
  184.6 2.1 fusion.37
  186.8 0.0 all-reduce.5.cloned.1.call-update
  186.8 0.0 all-reduce.7.cloned.1.call-start
  186.8 16.9 %all-reduce.5.cloned.1.call-done = f32[256,64]{0,1:T(8,128)} async-done(((f32[256,64]{0,1:T(8,128)}), f32[256,64]{0,1:T(8,128)}) %all-reduce.5.cloned.1.call-update) | async-done | bytes 65552 | tf_op jit(solution)/shard_map/psum | solution.py:96
  203.8 3.9 %convolution_multiply_fusion = f32[2048,64]{0,1:T(8,128)} fusion(f32[256,64]{0,1:T(8,128)} %all-reduce.5.cloned.1.call-done, f32[256,2048]{0,1:T(8,128)S(1)} %get-tuple-element.10, f32[2048]{0:T(1024)S(1)} %broadcast_multiply_fusion), kind=kOutput, calls=%fused_computation.6 | convolution fusion | flops 403308544 | bytes 2695168 | tf_op jit(solution)/shard_map/ck,cr->kr/dot_general | solution.py:98
  207.7 0.0 all-reduce.7.cloned.1.call-update
  207.7 0.0 copy-start.4
  207.7 0.6 dynamic-slice
  209.0 1.8 copy.15
  210.8 87.7 %all-reduce.7.cloned.1.call-done = f32[2048,64]{0,1:T(8,128)} async-done(((f32[2048,64]{0,1:T(8,128)}), f32[2048,64]{0,1:T(8,128)}) %all-reduce.7.cloned.1.call-update) | async-done | bytes 524304
  298.5 1.5 dynamic-slice_add_fusion
  300.0 0.6 copy.18
  (19 shorter events, 0.1 us)
Async XLA Ops:
  7.2 177.5 %copy-start = (f32[2048,64]{0,1:T(8,128)S(1)}, f32[2048,64]{0,1:T(8,128)}, u32[]{:S(2)}) copy-start(f32[2048,64]{0,1:T(8,128)} %param.6) | copy-start | bytes 1572868
  7.2 196.6 %all-reduce.5.cloned.1.call-start = ((), (), s32[]{:S(2)}) async-start(), calls=%async_computation | async-start | bytes 131072 | tf_op jit(solution)/shard_map/psum | solution.py:96
  119.1 9.0 %collective-permute-start.1 = (f32[256,3]{0,1:T(4,128)S(1)}, f32[256,3]{0,1:T(4,128)S(1)}, u32[]{:S(2)}, u32[]{:S(2)}) collective-permute-start(f32[256,3]{0,1:T(4,128)S(1)} %slice.196), channel_id=1, source_target_pairs={{0,1},{2,3},{4,5},{6,7},{8,9},{10,11},{12,13},{14,15},{16,17},{18,... | collective-permute-start | bytes 9224 | tf_op jit(solution)/shard_map/ppermute | solution.py:14
  124.7 5.7 %collective-permute-start = (f32[256,8]{0,1:T(8,128)S(1)}, f32[256,8]{0,1:T(8,128)S(1)}, u32[]{:S(2)}, u32[]{:S(2)}) collective-permute-start(f32[256,8]{0,1:T(8,128)S(1)} %slice.194), channel_id=1, source_target_pairs={{0,1},{2,3},{4,5},{6,7},{8,9},{10,11},{12,13},{14,15},{16,17},{18,... | collective-permute-start | bytes 24584 | tf_op jit(solution)/shard_map/ppermute | solution.py:22
  128.1 2.3 copy-start.1
  128.9 5.5 %collective-permute-start.2 = (f32[256,8]{0,1:T(8,128)S(1)}, f32[256,8]{0,1:T(8,128)S(1)}, u32[]{:S(2)}, u32[]{:S(2)}) collective-permute-start(f32[256,8]{0,1:T(8,128)S(1)} %fusion.41), channel_id=1, source_target_pairs={{1,0},{3,2},{5,4},{7,6},{9,8},{11,10},{13,12},{15,14},{17,16},{19,... | collective-permute-start | bytes 24584 | tf_op jit(solution)/shard_map/ppermute | solution.py:25
  139.7 1.2 copy-start.5
  148.6 1.6 copy-start.2
  186.8 21.0 %copy-start.6 = (u32[32]{0:T(128)S(1)}, u32[32]{0:T(128)}, u32[]{:S(2)}) copy-start(u32[32]{0:T(128)} %constant.48) | copy-start | bytes 388
  186.8 111.7 %all-reduce.7.cloned.1.call-start = ((), (), s32[]{:S(2)}) async-start(), calls=%async_computation.1 | async-start | bytes 1048576
  207.7 90.8 %copy-start.4 = (f32[2048,4]{0,1:T(4,128)S(1)}, f32[2048,4]{0,1:T(4,128)}, u32[]{:S(2)}) copy-start(f32[2048,4]{0,1:T(4,128)} %param.7) | copy-start | bytes 98308
  209.0 91.0 %copy-start.3 = (f32[256,64]{0,1:T(8,128)S(1)}, f32[256,64]{0,1:T(8,128)}, u32[]{:S(2)}) copy-start(f32[256,64]{0,1:T(8,128)} %all-reduce.5.cloned.1.call-done) | copy-start | bytes 196612
Sparse Core Ops, SparseCore 0:
  186.9 16.7 all-reduce.4
  207.8 90.6 all-reduce.6
where the time goes:
time: 309 us; the launch traced here: 307 us
  waiting for transfers between devices  109 us (35%)
  local copies, waits for them, and re-layouts  85.2 us (28%)
  blocking collectives  32.6 us (11%)
  other arithmetic  30.6 us (10%)
  matrix products  27.7 us (9%)
  between operations  15 us (5%)
  starting transfers between devices  7.68 us (2%)
    unnamed x3, waiting for transfers between devices  87.8 us
    unnamed x18, local copies, waits for them, and re-layouts  36.9 us
    reshape x1, local copies, waits for them, and re-layouts, body(): blocks = samples.reshape(row_count, basis_width, SPB)  35.7 us
    psum x1, blocking collectives, body(): totals = lax.psum(jnp.sum(coefficients, axis=0), 'curve')  32.6 us
    dot_general x1, matrix products, body(): jnp.einsum('cgq,mq->mcg', blocks, weight_table(), precision=lax.Precision...  21.7 us
    psum x1, waiting for transfers between devices, body(): scores = lax.psum(partial_value, 'tm')  16.9 us
    add x1, other arithmetic, body(): padded[0, :, 0:basis_width + 3] + padded[1, :, 1:basis_width + 4]  16.1 us
  transfers between devices with their start and end apart: 5, of which 3 were waited for; matrix products, arithmetic and copies ran while one was open for 2% of the time, Pallas kernels for 0%

commit v1 on v0

--- a/solution.py
+++ b/solution.py
@@ -87,7 +87,7 @@
         target = proj_wide[:, offset : offset + basis_width + 2 * margin_now - 4]
         coefficients = relax_sweep(coefficients, target, smooth_col, index_wide, total_basis)
     curve_total = row_count * lax.axis_size("curve")
-    totals = lax.psum(jnp.sum(coefficients, axis=0), "curve")
+    totals = jnp.sum(lax.all_gather(jnp.sum(coefficients, axis=0), "curve"), axis=0)
     column_mean = totals / curve_total
     centered = coefficients - column_mean[None, :]
     partial_value = jnp.dot(

time: 309 us -> 299 us (0.968)
  blocking collectives: 32.6 us -> 22 us
    psum x1 -> x0, blocking collectives: 32.6 us -> none  [body(): totals = lax.psum(jnp.sum(coefficients, axis=0), 'curve')]
    all_gather x0 -> x1, blocking collectives: none -> 22 us  [body(): lax.all_gather(jnp.sum(coefficients, axis=0), 'curve')]
where the time goes in v1:
time: 299 us; the launch traced here: 297 us
  waiting for transfers between devices  109 us (36%)
  local copies, waits for them, and re-layouts  85.2 us (28%)
  other arithmetic  30.7 us (10%)
  matrix products  27.7 us (9%)
  blocking collectives  22 us (7%)
  between operations  15 us (5%)
  starting transfers between devices  7.68 us (3%)
    unnamed x3, waiting for transfers between devices  87.8 us
    unnamed x18, local copies, waits for them, and re-layouts  36.9 us
    reshape x1, local copies, waits for them, and re-layouts, body(): blocks = samples.reshape(row_count, basis_width, SPB)  35.7 us
    all_gather x1, blocking collectives, body(): lax.all_gather(jnp.sum(coefficients, axis=0), 'curve')  22 us
    dot_general x1, matrix products, body(): jnp.einsum('cgq,mq->mcg', blocks, weight_table(), precision=lax.Precision...  21.7 us
    psum x1, waiting for transfers between devices, body(): scores = lax.psum(partial_value, 'tm')  17.2 us
    add x1, other arithmetic, body(): padded[0, :, 0:basis_width + 3] + padded[1, :, 1:basis_width + 4]  16.1 us
  transfers between devices with their start and end apart: 5, of which 3 were waited for; matrix products, arithmetic and copies ran while one was open for 2% of the time, Pallas kernels for 0%

profile of v1, /device:TPU:0, one launch (start us, length us, event | category | flops | bytes accessed | tf_op | source)
XLA Modules:
  0.0 297.2 jit_solution(15883552816267919948)
XLA Ops:
  7.2 0.0 copy-start
  7.2 0.0 all-reduce.5.cloned.1.call-start
  7.3 33.5 %copy.16 = f32[256,32768]{0,1:T(8,128)} copy(f32[256,32768]{1,0:T(8,128)} %param.4) | data formatting | bytes 67108864 | tf_op args[0]
  40.7 35.7 %copy.17 = f32[256,2048,16]{1,2,0:T(8,128)} copy(f32[256,2048,16]{0,2,1:T(8,128)} %bitcast.9) | data formatting | bytes 67108864 | tf_op jit(solution)/shard_map/reshape | solution.py:61
  76.4 21.7 %fusion.43 = f32[4,256,2048]{2,0,1:T(4,128)S(1)} fusion(f32[256,2048,16]{1,2,0:T(8,128)} %copy.17, f32[1,16]{1,0:T(1,128)S(1)} %get-tuple-element.14, f32[1,16]{1,0:T(1,128)S(1)} %get-tuple-element.15, f32[1,16]{1,0:T(1,128)S(1)} %get-tuple-element.16, f32[1,16]{1,0:T(1,128)S(1)} %get-tuple-element.17), kind=kOutput, calls=%fused_computation.85 | convolution fusion | flops 402653440 | bytes 41943296 | tf_op jit(solution)/shard_map/cgq,mq->mcg/dot_general | solution.py:62
  98.1 16.1 %fusion.2 = f32[1,256,2051]{2,0,1:T(1,128)S(1)} fusion(f32[4,256,2048]{2,0,1:T(4,128)S(1)} %fusion.43), kind=kLoop, calls=%fused_computation.9 | loop fusion | flops 1575168 | bytes 10488832 | tf_op jit(solution)/shard_map/add | solution.py:67
  114.3 4.1 %copy.18 = f32[1,256,2051]{1,2,0:T(8,128)} copy(f32[1,256,2051]{2,0,1:T(1,128)S(1)} %fusion.2) | data formatting | bytes 4200448 | tf_op jit(solution)/shard_map/add | solution.py:67
  118.4 0.7 slice.196
  119.1 4.9 %collective-permute-start.1 = (f32[256,3]{0,1:T(4,128)S(1)}, f32[256,3]{0,1:T(4,128)S(1)}, u32[]{:S(2)}, u32[]{:S(2)}) collective-permute-start(f32[256,3]{0,1:T(4,128)S(1)} %slice.196), channel_id=1, source_target_pairs={{0,1},{2,3},{4,5},{6,7},{8,9},{10,11},{12,13},{14,15},{16,17},{18,... | collective-permute-start | bytes 9224 | tf_op jit(solution)/shard_map/ppermute | solution.py:14
  124.0 0.7 slice.194
  124.7 1.3 collective-permute-start
  126.0 0.1 convert_add_fusion.2
  126.1 0.1 convert_add_fusion.1
  126.2 0.1 convert_add_fusion
  126.3 0.1 convert_add_fusion.3
  126.3 1.7 slice.197
  128.1 0.0 copy-start.1
  128.1 0.0 collective-permute-done.1
  128.1 0.7 slice_add_fusion.8
  128.9 1.5 collective-permute-start.2
  130.3 0.0 collective-permute-done
  130.4 0.0 copy-done.1
  130.4 4.0 %collective-permute-done.2 = f32[256,8]{0,1:T(8,128)S(1)} collective-permute-done((f32[256,8]{0,1:T(8,128)S(1)}, f32[256,8]{0,1:T(8,128)S(1)}, u32[]{:S(2)}, u32[]{:S(2)}) %collective-permute-start.2) | collective-permute-done | bytes 8224 | tf_op jit(solution)/shard_map/ppermute | solution.py:25
  134.4 5.3 %concatenate.8 = f32[256,2064]{0,1:T(8,128)S(1)} concatenate(f32[256,8]{0,1:T(8,128)S(1)} %collective-permute-done, f32[256,3]{0,1:T(4,128)S(1)} %slice_add_fusion.8, f32[256,2045]{0,1:T(8,128)} %copy-done.1, f32[256,8]{0,1:T(8,128)S(1)} %collective-permute-done.2), dimensions={1} | concatenate | bytes 4227072 | tf_op jit(solution)/shard_map/concatenate | solution.py:26
  139.7 0.0 copy-start.5
  139.7 1.2 fusion.11
  140.9 1.7 fusion.9
  142.6 1.2 fusion.3
  143.8 1.8 fusion.27
  145.6 1.2 fusion.21
  146.8 1.8 fusion.19
  148.6 0.0 copy-start.2
  148.6 1.2 fusion.13
  149.8 0.4 copy-done.2
  150.2 1.8 fusion.56
  152.1 22.0 %all-gather = f32[32768]{0:T(1024)S(1)} all-gather(f32[2048]{0:T(1024)S(1)} %get-tuple-element.12), channel_id=2, replica_groups=mesh['curve'=16,'tm'=2] {'curve'}, dimensions={0}, use_global_device_ids=true | all-gather | bytes 139264 | tf_op jit(solution)/shard_map/all_gather | solution.py:90
  174.1 2.1 fusion.37
  176.3 0.0 all-reduce.5.cloned.1.call-update
  176.3 0.0 all-reduce.7.cloned.1.call-start
  176.3 17.2 %all-reduce.5.cloned.1.call-done = f32[256,64]{0,1:T(8,128)} async-done(((f32[256,64]{0,1:T(8,128)}), f32[256,64]{0,1:T(8,128)}) %all-reduce.5.cloned.1.call-update) | async-done | bytes 65552 | tf_op jit(solution)/shard_map/psum | solution.py:96
  193.5 3.9 %convolution_multiply_fusion = f32[2048,64]{0,1:T(8,128)} fusion(f32[256,64]{0,1:T(8,128)} %all-reduce.5.cloned.1.call-done, f32[256,2048]{0,1:T(8,128)S(1)} %get-tuple-element.13, f32[2048]{0:T(1024)S(1)} %broadcast_multiply_fusion), kind=kOutput, calls=%fused_computation.6 | convolution fusion | flops 403308544 | bytes 2695168 | tf_op jit(solution)/shard_map/ck,cr->kr/dot_general | solution.py:98
  197.4 0.0 all-reduce.7.cloned.1.call-update
  197.5 0.0 copy-start.4
  197.5 0.6 dynamic-slice
  198.7 1.8 copy.19
  200.5 87.7 %all-reduce.7.cloned.1.call-done = f32[2048,64]{0,1:T(8,128)} async-done(((f32[2048,64]{0,1:T(8,128)}), f32[2048,64]{0,1:T(8,128)}) %all-reduce.7.cloned.1.call-update) | async-done | bytes 524304
  288.3 1.5 dynamic-slice_add_fusion
  289.7 0.6 copy.22
  (21 shorter events, 0.2 us)
Async XLA Ops:
  7.2 167.0 %copy-start = (f32[2048,64]{0,1:T(8,128)S(1)}, f32[2048,64]{0,1:T(8,128)}, u32[]{:S(2)}) copy-start(f32[2048,64]{0,1:T(8,128)} %param.6) | copy-start | bytes 1572868
  7.2 186.3 %all-reduce.5.cloned.1.call-start = ((), (), s32[]{:S(2)}) async-start(), calls=%async_computation | async-start | bytes 131072 | tf_op jit(solution)/shard_map/psum | solution.py:96
  119.1 9.0 %collective-permute-start.1 = (f32[256,3]{0,1:T(4,128)S(1)}, f32[256,3]{0,1:T(4,128)S(1)}, u32[]{:S(2)}, u32[]{:S(2)}) collective-permute-start(f32[256,3]{0,1:T(4,128)S(1)} %slice.196), channel_id=1, source_target_pairs={{0,1},{2,3},{4,5},{6,7},{8,9},{10,11},{12,13},{14,15},{16,17},{18,... | collective-permute-start | bytes 9224 | tf_op jit(solution)/shard_map/ppermute | solution.py:14
  124.7 5.7 %collective-permute-start = (f32[256,8]{0,1:T(8,128)S(1)}, f32[256,8]{0,1:T(8,128)S(1)}, u32[]{:S(2)}, u32[]{:S(2)}) collective-permute-start(f32[256,8]{0,1:T(8,128)S(1)} %slice.194), channel_id=1, source_target_pairs={{0,1},{2,3},{4,5},{6,7},{8,9},{10,11},{12,13},{14,15},{16,17},{18,... | collective-permute-start | bytes 24584 | tf_op jit(solution)/shard_map/ppermute | solution.py:22
  128.1 2.3 copy-start.1
  128.9 5.5 %collective-permute-start.2 = (f32[256,8]{0,1:T(8,128)S(1)}, f32[256,8]{0,1:T(8,128)S(1)}, u32[]{:S(2)}, u32[]{:S(2)}) collective-permute-start(f32[256,8]{0,1:T(8,128)S(1)} %fusion.41), channel_id=1, source_target_pairs={{1,0},{3,2},{5,4},{7,6},{9,8},{11,10},{13,12},{15,14},{17,16},{19,... | collective-permute-start | bytes 24584 | tf_op jit(solution)/shard_map/ppermute | solution.py:25
  139.7 1.2 copy-start.5
  148.6 1.6 copy-start.2
  176.3 21.2 %copy-start.6 = (u32[32]{0:T(128)S(1)}, u32[32]{0:T(128)}, u32[]{:S(2)}) copy-start(u32[32]{0:T(128)} %constant.48) | copy-start | bytes 388
  176.3 112.0 %all-reduce.7.cloned.1.call-start = ((), (), s32[]{:S(2)}) async-start(), calls=%async_computation.1 | async-start | bytes 1048576
  197.5 90.8 %copy-start.4 = (f32[2048,4]{0,1:T(4,128)S(1)}, f32[2048,4]{0,1:T(4,128)}, u32[]{:S(2)}) copy-start(f32[2048,4]{0,1:T(4,128)} %param.7) | copy-start | bytes 98308
  198.7 91.0 %copy-start.3 = (f32[256,64]{0,1:T(8,128)S(1)}, f32[256,64]{0,1:T(8,128)}, u32[]{:S(2)}) copy-start(f32[256,64]{0,1:T(8,128)} %all-reduce.5.cloned.1.call-done) | copy-start | bytes 196612
Sparse Core Ops, SparseCore 0:
  176.4 17.0 all-reduce.4
  197.6 90.6 all-reduce.6
